TPU v7x, 32 devices: a whole 2x2x4 slice. The times are simulated.
32 devices in a mesh: seq: 8 (over y, x, core), tp: 4 (over z).
Axes of the slice: x: 2, y: 2, z: 4, core: 2. Of those that a mesh axis runs over, the one named last changes fastest.
Arguments:
- hidden: bfloat16 [8192, 2560], P('seq', 'tp'), may hold values from -6 to 6
- gate_proj: bfloat16 [2560, 5120], P(None, 'tp'), may hold values from -0.125 to 0.125
- input_proj: bfloat16 [2560, 5120], P(None, 'tp'), may hold values from -0.125 to 0.125
- bc_proj: bfloat16 [2560, 256], replicated, may hold values from -0.125 to 0.125
- step_proj: bfloat16 [2560, 80], P(None, 'tp'), may hold values from -0.125 to 0.125
- step_bias: float32 [80], P('tp'), may hold values from -16 to -3
- decay_log: float32 [80], P('tp'), may hold values from 0 to 2.78
- conv_weight: float32 [4, 5120], P(None, 'tp'), may hold values from -3 to 3
- conv_bias: float32 [5120], P('tp'), may hold values from -3 to 3
- bc_conv_weight: float32 [4, 256], replicated, may hold values from -3 to 3
- bc_conv_bias: float32 [256], replicated, may hold values from -3 to 3
- skip_gain: float32 [80], P('tp'), may hold values from 0.5 to 2
- norm_gain: float32 [5120], P('tp'), may hold values from 0.1 to 1.9
- out_proj: bfloat16 [5120, 2560], P('tp'), may hold values from -0.078125 to 0.078125
- amax_history: float32 [16], replicated, may hold values from 1.5 to 4
Outputs:
- mixed: bfloat16 [8192, 2560], P('seq', 'tp')
- new_history: float32 [16], replicated
All inputs are finite; a program needn't handle non-finite values.
Results may differ from a plain program's by a relative error of at most 0.015.
Values may be sent and summed in bfloat16 or wider, within the bound.
A program may use at most 192 MiB of HBM per device.

v0:
```python
import jax
import jax.numpy as jnp
from jax import lax
from jax.sharding import PartitionSpec as P

BLOCK = 256
INNER = 5120
QMAX = 448.0
EPS = 1e-05


def shifted(x, axis, by):
    size = lax.axis_size(axis)
    pairs = [(i, i + by) for i in range(size) if 0 <= i + by < size]
    return lax.ppermute(x, axis, pairs)


def carried_in(x, axis, join, neutral):
    place = lax.axis_index(axis)
    gathered = jax.tree.map(
        lambda a, kind: lax.all_gather(a.astype(kind), axis), x, (jnp.bfloat16, jnp.bfloat16)
    )
    state = jax.tree.map(lambda a, e: jnp.zeros_like(a) + jnp.asarray(e, a.dtype), x, neutral)

    def one(turn, state):
        return join(
            state,
            jax.tree.map(
                lambda a, own: lax.dynamic_index_in_dim(a, turn, 0, False).astype(own.dtype),
                gathered,
                x,
            ),
        )

    return lax.fori_loop(0, place, one, state)


def conv_silu(pre_conv, rim_rows, weight, conv_shift):
    row_count = pre_conv.shape[0]
    kernel = weight.shape[0]
    padded = jnp.concatenate([rim_rows, pre_conv], axis=0)
    running = jnp.zeros(pre_conv.shape, jnp.float32)
    for offset in range(kernel):
        running = running + weight[offset] * padded[offset : offset + row_count].astype(jnp.float32)
    return jax.nn.silu(running + conv_shift).astype(jnp.bfloat16)


def ssd_block(carry_state, block_data):
    x_block, b_block, c_block, step_block, decay_block = block_data
    length = x_block.shape[0]
    head_count = carry_state.shape[0]
    head_width = carry_state.shape[1]
    cum_decay = jnp.cumsum(decay_block, axis=1)
    scores = jnp.dot(c_block, b_block.T, preferred_element_type=jnp.float32)
    causal = lax.broadcasted_iota(jnp.int32, (length, length), 0) >= lax.broadcasted_iota(
        jnp.int32, (length, length), 1
    )
    decay_gap = cum_decay[:, :, None] - cum_decay[:, None, :]
    decay_mask = jnp.where(causal, jnp.exp(jnp.where(causal, decay_gap, 0.0)), 0.0)
    weights = (scores[None] * decay_mask * step_block[:, None, :]).astype(jnp.bfloat16)
    x_heads = x_block.reshape(length, head_count, head_width)
    intra_out = jnp.einsum("hts,shp->htp", weights, x_heads, preferred_element_type=jnp.float32)
    inter_out = jnp.exp(cum_decay)[:, :, None] * jnp.einsum(
        "tn,hpn->htp", c_block.astype(jnp.float32), carry_state, precision=lax.Precision.HIGHEST
    )
    tail_decay = jnp.exp(cum_decay[:, -1:] - cum_decay) * step_block
    x_weighted = (tail_decay.T[:, :, None] * x_heads.astype(jnp.float32)).astype(jnp.bfloat16)
    update = jnp.einsum("shp,sn->hpn", x_weighted, b_block, preferred_element_type=jnp.float32)
    next_state = jnp.exp(cum_decay[:, -1])[:, None, None] * carry_state + update
    block_out = (intra_out + inter_out).transpose(1, 0, 2).reshape(length, head_count * head_width)
    return (next_state, block_out)


def chain(earlier, later):
    return (earlier[0] + later[0], jnp.exp(later[0])[..., None, None] * earlier[1] + later[1])


def shards(
    hidden,
    gate_proj,
    input_proj,
    bc_proj,
    step_proj,
    step_bias,
    decay_log,
    conv_weight,
    conv_bias,
    bc_conv_weight,
    bc_conv_bias,
    skip_gain,
    norm_gain,
    out_proj,
    amax_history,
):
    row_count = hidden.shape[0]
    inner_local = gate_proj.shape[1]
    state_width = bc_proj.shape[1] // 2
    head_count = step_proj.shape[1]
    head_width = inner_local // head_count
    kernel = conv_weight.shape[0]
    matrices = (gate_proj, input_proj, bc_proj, step_proj)
    piece = lax.all_gather(hidden, "tp", axis=1, tiled=True)
    gate_raw, x_raw, bc_raw, step_raw = tuple(
        (jnp.dot(piece, matrix, preferred_element_type=jnp.float32) for matrix in matrices)
    )
    gate_in = gate_raw.astype(jnp.bfloat16)
    x_pre = x_raw.astype(jnp.bfloat16)
    bc_pre = bc_raw.astype(jnp.bfloat16)
    x_rim, bc_rim = shifted(
        (x_pre[row_count - kernel + 1 :], bc_pre[row_count - kernel + 1 :]), "seq", 1
    )
    x_conv = conv_silu(x_pre, x_rim, conv_weight, conv_bias)
    bc_conv = conv_silu(bc_pre, bc_rim, bc_conv_weight, bc_conv_bias)
    b_in = bc_conv[:, :state_width]
    c_out = bc_conv[:, state_width:]
    step_size = jax.nn.softplus(step_raw + step_bias)
    log_decay = step_size * -jnp.exp(decay_log)
    blocks = row_count // BLOCK
    stacked = (
        x_conv.reshape(blocks, BLOCK, inner_local),
        b_in.reshape(blocks, BLOCK, state_width),
        c_out.reshape(blocks, BLOCK, state_width),
        step_size.reshape(blocks, BLOCK, head_count).transpose(0, 2, 1),
        log_decay.reshape(blocks, BLOCK, head_count).transpose(0, 2, 1),
    )
    zero_state = jnp.zeros((head_count, head_width, state_width), jnp.float32)
    local_state, block_outs = lax.scan(ssd_block, zero_state, stacked)
    total_decay = jnp.sum(log_decay, axis=0)
    entry_decay, incoming = carried_in(
        (total_decay, local_state), "seq", chain, (jnp.zeros_like(total_decay), zero_state)
    )
    reach = jnp.exp(jnp.cumsum(log_decay, axis=0))
    carried = jnp.einsum(
        "tn,hpn->thp", c_out.astype(jnp.float32), incoming, precision=lax.Precision.HIGHEST
    )
    ssm_out = block_outs.reshape(row_count, inner_local) + (reach[:, :, None] * carried).reshape(
        row_count, inner_local
    )
    x_heads = x_conv.reshape(row_count, head_count, head_width).astype(jnp.float32)
    ssm_out = ssm_out + (skip_gain[:, None] * x_heads).reshape(row_count, inner_local)
    gated = ssm_out * jax.nn.silu(gate_in.astype(jnp.float32))
    local_squares = jnp.sum(gated * gated, axis=1)
    squares = lax.psum(local_squares, "tp")
    inv_rms = lax.rsqrt(squares / INNER + EPS)
    normed = gated * inv_rms[:, None] * norm_gain
    peak_value = lax.pmax(jnp.max(jnp.abs(normed)), ("seq", "tp"))
    scale = QMAX / jnp.max(amax_history)
    quant = jnp.clip(normed * scale, -QMAX, QMAX).astype(jnp.bfloat16)
    partial_value = jnp.dot(quant, out_proj, preferred_element_type=jnp.float32)
    summed = lax.psum_scatter(
        partial_value.astype(jnp.bfloat16), "tp", scatter_dimension=1, tiled=True
    ).astype(jnp.float32)
    mixed = (summed / scale).astype(jnp.bfloat16)
    new_history = jnp.concatenate([jnp.reshape(peak_value, (1,)), amax_history[:-1]])
    return (mixed, new_history)


def solution(mesh):
    return jax.shard_map(
        shards,
        mesh=mesh,
        in_specs=(
            P("seq", "tp"),
            P(None, "tp"),
            P(None, "tp"),
            P(),
            P(None, "tp"),
            P("tp"),
            P("tp"),
            P(None, "tp"),
            P("tp"),
            P(),
            P(),
            P("tp"),
            P("tp"),
            P("tp", None),
            P(),
        ),
        out_specs=(P("seq", "tp"), P()),
        check_vma=False,
    )
```

profile of v0, /device:TPU:0, one launch (start us, length us, event | category | flops | bytes accessed | tf_op | source)
XLA Modules:
  0.0 387.2 jit_solution(16911178018496801252)
XLA Ops:
  10.4 100.0 %all-gather.5.cloned.1.call-done = bf16[1024,2560]{1,0:T(8,128)(2,1)} async-done(((bf16[1024,640]{1,0:T(8,128)(2,1)}), bf16[1024,2560]{1,0:T(8,128)(2,1)}) %all-gather.5.cloned.1.call-update) | async-done | bytes 5242896 | tf_op jit(solution)/shard_map/all_gather | solution.py:102
  110.4 4.1 %convolution_convert_fusion.3 = bf16[1024,256]{1,0:T(8,128)(2,1)S(1)} fusion(bf16[1024,2560]{1,0:T(8,128)(2,1)} %all-gather.5.cloned.1.call-done, bf16[2560,256]{1,0:T(8,128)(2,1)S(1)} %copy-done), kind=kOutput, calls=%fused_computation.71 | convolution fusion | flops 1342439424 | bytes 7077888 | tf_op jit(solution)/shard_map/dot_general | solution.py:104
  114.6 1.9 collective-permute-start.1
  116.5 10.0 %convolution_convert_fusion.2 = bf16[1024,1280]{1,0:T(8,128)(2,1)S(1)} fusion(bf16[1024,2560]{1,0:T(8,128)(2,1)S(1)} %copy-done.3, bf16[2560,1280]{1,0:T(8,128)(2,1)} %param.21), kind=kOutput, calls=%fused_computation.58 | convolution fusion | flops 6712197120 | bytes 14417920 | tf_op jit(solution)/shard_map/dot_general | solution.py:104
  126.5 3.8 collective-permute-start
  130.3 2.2 fusion.42
  134.3 8.2 %multiply_convert_fusion.4 = bf16[1024,1280]{1,0:T(8,128)(2,1)} fusion(bf16[1024,1280]{1,0:T(8,128)(2,1)} %copy-done.8, bf16[3,1280]{1,0:T(4,128)(2,1)S(1)} %collective-permute-done, f32[1280]{0:T(1024)S(1)} %copy-done.10, f32[1280]{0:T(1024)S(1)} %get-tuple-element.153, f32[1280]{0:T(1024)S(1)} %get-tuple-element.154, f32[1280]{0:T(1024)S(1)} %get-tuple-element.152, ...), kind=kLoop, calls=%fused_computation.56 | loop fusion | flops 34078720 | bytes 5276160 | tf_op jit(solution)/shard_map/convert_element_type | solution.py:45
  142.5 48.7 %while.26 = (s32[]{:T(128)}, f32[20,64,128]{2,1,0:T(8,128)S(1)}, f32[4,256,1280]{2,1,0:T(8,128)}, f32[4,20,256]{2,1,0:T(8,128)}, f32[4,20,256]{2,1,0:T(8,128)}, ...) while((s32[]{:T(128)}, f32[20,64,128]{2,1,0:T(8,128)S(1)}, ...), condition=%wide.region_3.4_spmd.clone, body=%wide.region_0.3_spmd.clone.sunk | while | flops 782641216 | bytes 22548344 | solution.py:127
  144.5 1.4 multiply_bitcast_fusion.2
  147.5 1.7 fusion.85
  149.2 1.4 fusion.86
  156.7 1.4 multiply_bitcast_fusion.2
  159.7 1.7 fusion.85
  161.4 1.4 fusion.86
  168.8 1.4 multiply_bitcast_fusion.2
  171.8 1.7 fusion.85
  173.5 1.4 fusion.86
  184.1 1.7 fusion.85
  185.8 1.4 fusion.86
  195.8 12.1 %all-reduce = bf16[160]{0:T(256)(128)(2,1)S(1)} all-reduce(bf16[160]{0:T(256)(128)(2,1)S(1)} %dynamic-update-slice), channel_id=2, replica_groups=mesh['seq'=8,'tp'=4] {'seq'}, use_global_device_ids=true, to_apply=%add | all-reduce | flops 160 | bytes 640
  208.9 5.6 %reduce-window.16 = f32[20,8,128]{2,1,0:T(8,128)S(1)} reduce-window(f32[20,8,128]{2,1,0:T(8,128)S(1)} %slice.113, f32[]{:T(128)} %constant.62.clone.1), window={size=1x1x128 pad=0_0x0_0x127_0}, to_apply=%region_4.5 | reduce-window | flops 2600960 | bytes 163844 | tf_op jit(solution)/shard_map/reduce-window.2
  215.0 4.7 %all-gather.7.cloned.1.call-done = bf16[160,64,128]{2,1,0:T(8,128)(2,1)} async-done(((bf16[20,64,128]{2,1,0:T(8,128)(2,1)}), bf16[160,64,128]{2,1,0:T(8,128)(2,1)}) %all-gather.7.cloned.1.call-update) | async-done | bytes 2621456 | tf_op jit(solution)/shard_map/all_gather | solution.py:21
  219.8 4.6 %broadcast_multiply_fusion = f32[1024,20,64]{0,2,1:T(8,128)} fusion(f32[1024,20]{0,1:T(8,128)S(1)} %bitcast.151, f32[20,64,128]{2,1,0:T(8,128)S(1)} %get-tuple-element.91, bf16[1024,256]{1,0:T(8,128)(2,1)S(1)} %copy-done.5), kind=kOutput, calls=%fused_computation.69 | convolution fusion | flops 2014576640 | bytes 6258688 | tf_op jit(solution)/shard_map/tn,hpn->thp/dot_general | solution.py:133
  224.4 5.9 %copy.53 = f32[1024,1280]{1,0:T(8,128)} copy(f32[1024,1280]{0,1:T(8,128)} %bitcast.139) | data formatting | bytes 10485760 | tf_op jit(solution)/shard_map/reshape | solution.py:136
  230.2 15.6 %multiply_reduce_fusion = (f32[1024]{0:T(1024)S(1)}, f32[1024,1280]{1,0:T(8,128)}) fusion(bf16[1024,2560]{1,0:T(8,128)(2,1)} %all-gather.5.cloned.1.call-done, bf16[2560,1280]{1,0:T(8,128)(2,1)} %param.20, bf16[1024,1280]{1,0:T(8,128)(2,1)} %bitcast.142, f32[1280]{0:T(1024)S(1)} %mul.247, f32[1024,1280]{1,0:T(8,128)} %copy.53, ...), kind=kOutput, calls=%fused_computation.55 | convolution fusion | flops 6727924736 | bytes 30155776 | tf_op jit(solution)/shard_map/dot_general | solution.py:104
  245.8 11.7 %psum.7 = f32[1024]{0:T(1024)S(1)} all-reduce(f32[1024]{0:T(1024)S(1)} %get-tuple-element.195), channel_id=1, replica_groups=mesh['seq'=8,'tp'=4] {'tp'}, use_global_device_ids=true, to_apply=%region_10.11 | all-reduce | flops 1024 | bytes 8192 | tf_op jit(solution)/shard_map/psum | solution.py:143
  257.5 12.8 %convolution_convert_fusion = bf16[1024,2560]{1,0:T(8,128)(2,1)} fusion(bf16[1280,2560]{1,0:T(8,128)(2,1)} %param.32, f32[1024,1280]{1,0:T(8,128)} %get-tuple-element.196, f32[]{:T(128)S(6)} %div.31, f32[1280]{0:T(1024)S(1)} %copy-done.11, f32[1024]{0:T(1024)S(1)} %add_rsqrt_fusion), kind=kOutput, calls=%fused_computation.45 | convolution fusion | flops 6720061440 | bytes 17048580 | tf_op jit(solution)/shard_map/dot_general | solution.py:149
  270.3 8.0 %copy.54 = bf16[1024,2560]{0,1:T(8,128)(2,1)} copy(bf16[1024,2560]{1,0:T(8,128)(2,1)} %convolution_convert_fusion) | data formatting | bytes 10485760
  278.3 4.0 %abs_reduce_fusion = f32[]{:T(128)} fusion(f32[1024,1280]{1,0:T(8,128)} %get-tuple-element.196, f32[1280]{0:T(1024)S(1)} %copy-done.11, f32[1024]{0:T(1024)S(1)} %add_rsqrt_fusion), kind=kLoop, calls=%fused_computation.52 | loop fusion | flops 5242879 | bytes 5252100 | tf_op jit(solution)/shard_map/reduce_max | solution.py:146
  282.2 51.0 %pmax.7 = f32[1]{0:T(128)} all-reduce(f32[1]{0:T(128)} %bitcast.19), channel_id=1, replica_groups=mesh['seq'=8,'tp'=4] {'seq','tp'}, use_global_device_ids=true, to_apply=%region_14.15 | all-reduce | flops 1 | bytes 8 | tf_op jit(solution)/shard_map/pmax | solution.py:146
  334.5 43.2 %reduce-scatter.4.cloned.1.call-done = bf16[640,1024]{1,0:T(8,128)(2,1)} async-done(((bf16[2560,1024]{1,0:T(8,128)(2,1)}), bf16[640,1024]{1,0:T(8,128)(2,1)}) %reduce-scatter.4.cloned.1.call-update) | async-done | bytes 1310736
  377.7 1.7 copy.55
  (179 shorter events, 43.8 us)
Async XLA Ops:
  7.2 103.2 %copy-start = (bf16[2560,256]{1,0:T(8,128)(2,1)S(1)}, bf16[2560,256]{1,0:T(8,128)(2,1)}, u32[]{:S(2)}) copy-start(bf16[2560,256]{1,0:T(8,128)(2,1)} %param.22) | copy-start | bytes 3932164
  7.2 103.2 %all-gather.5.cloned.1.call-start = ((), (), s32[]{:S(2)}) async-start(), calls=%async_computation.1 | async-start | bytes 6553600 | tf_op jit(solution)/shard_map/all_gather | solution.py:102
  7.9 211.8 %all-gather.7.cloned.1.call-start = ((), (), s32[]{:S(2)}) async-start(), calls=%async_computation.2 | async-start | bytes 2949120 | tf_op jit(solution)/shard_map/all_gather | solution.py:21
  110.4 6.1 %copy-start.3 = (bf16[1024,2560]{1,0:T(8,128)(2,1)S(1)}, bf16[1024,2560]{1,0:T(8,128)(2,1)}, u32[]{:S(2)}) copy-start(bf16[1024,2560]{1,0:T(8,128)(2,1)} %all-gather.5.cloned.1.call-done) | copy-start | bytes 15728644
  114.6 15.8 %copy-start.9 = (bf16[2560,20]{0,1:T(8,128)(2,1)S(1)}, bf16[2560,20]{0,1:T(8,128)(2,1)}, u32[]{:S(2)}) copy-start(bf16[2560,20]{0,1:T(8,128)(2,1)} %param.23) | copy-start | bytes 307204
  114.6 15.8 %copy-start.12 = (f32[20]{0:T(128)S(1)}, f32[20]{0:T(128)}, u32[]{:S(2)}) copy-start(f32[20]{0:T(128)} %param.24) | copy-start | bytes 244
  114.6 18.9 %collective-permute-start.1 = (bf16[3,256]{1,0:T(4,128)(2,1)S(1)}, bf16[3,256]{1,0:T(4,128)(2,1)S(1)}, u32[]{:S(2)}, u32[]{:S(2)}) collective-permute-start(bf16[3,256]{1,0:T(4,128)(2,1)S(1)} %slice.104), channel_id=1, source_target_pairs={{0,4},{4,8},{8,12},{12,16},{16,20},{20,24},{24,28},{1,5},{5,9},{9,... | collective-permute-start | bytes 4616 | tf_op jit(solution)/shard_map/ppermute | solution.py:15
  126.5 6.0 %copy-start.8 = (bf16[1024,1280]{1,0:T(8,128)(2,1)}, bf16[1024,1280]{1,0:T(8,128)(2,1)S(1)}, u32[]{:S(2)}) copy-start(bf16[1024,1280]{1,0:T(8,128)(2,1)S(1)} %convolution_convert_fusion.2) | copy-start | bytes 7864324
  126.5 7.0 %copy-start.13 = (f32[256]{0:T(256)S(1)}, f32[256]{0:T(256)}, u32[]{:S(2)}) copy-start(f32[256]{0:T(256)} %param.29) | copy-start | bytes 3076
  126.5 7.8 %copy-start.10 = (f32[1280]{0:T(1024)S(1)}, f32[1280]{0:T(1024)}, u32[]{:S(2)}) copy-start(f32[1280]{0:T(1024)} %param.27) | copy-start | bytes 15364
  126.5 7.7 %collective-permute-start = (bf16[3,1280]{1,0:T(4,128)(2,1)S(1)}, bf16[3,1280]{1,0:T(4,128)(2,1)S(1)}, u32[]{:S(2)}, u32[]{:S(2)}) collective-permute-start(bf16[3,1280]{1,0:T(4,128)(2,1)S(1)} %slice.99), channel_id=1, source_target_pairs={{0,4},{4,8},{8,12},{12,16},{16,20},{20,24},{24,28},{1,5},{5,9},{9,... | collective-permute-start | bytes 23048 | tf_op jit(solution)/shard_map/ppermute | solution.py:15
  134.2 8.3 %copy-start.4 = (bf16[1024,256]{1,0:T(8,128)(2,1)}, bf16[1024,256]{1,0:T(8,128)(2,1)S(1)}, u32[]{:S(2)}) copy-start(bf16[1024,256]{1,0:T(8,128)(2,1)S(1)} %multiply_convert_fusion.5) | copy-start | bytes 1572868
  142.5 49.8 %copy-start.14 = (f32[20]{0:T(128)S(1)}, f32[20]{0:T(128)}, u32[]{:S(2)}) copy-start(f32[20]{0:T(128)} %param.30) | copy-start | bytes 244
  142.5 51.7 %copy-start.15 = (f32[16]{0:T(128)S(1)}, f32[16]{0:T(128)}, u32[]{:S(2)}) copy-start(f32[16]{0:T(128)} %param.33) | copy-start | bytes 196
  142.5 6.7 %copy-start.6 = (bf16[4,256,128]{2,1,0:T(8,128)(2,1)}, bf16[4,256,128]{2,1,0:T(8,128)(2,1)S(1)}, u32[]{:S(2)}) copy-start(bf16[4,256,128]{2,1,0:T(8,128)(2,1)S(1)} %get-tuple-element.314) | copy-start | bytes 786436 | tf_op jit(solution)/shard_map/while
  147.5 1.7 copy-start.2
  151.1 3.6 copy-start.7
  154.7 6.7 %copy-start.6 = (bf16[4,256,128]{2,1,0:T(8,128)(2,1)}, bf16[4,256,128]{2,1,0:T(8,128)(2,1)S(1)}, u32[]{:S(2)}) copy-start(bf16[4,256,128]{2,1,0:T(8,128)(2,1)S(1)} %get-tuple-element.314) | copy-start | bytes 786436 | tf_op jit(solution)/shard_map/while
  159.7 1.7 copy-start.2
  163.2 3.6 copy-start.7
  166.9 6.7 %copy-start.6 = (bf16[4,256,128]{2,1,0:T(8,128)(2,1)}, bf16[4,256,128]{2,1,0:T(8,128)(2,1)S(1)}, u32[]{:S(2)}) copy-start(bf16[4,256,128]{2,1,0:T(8,128)(2,1)S(1)} %get-tuple-element.314) | copy-start | bytes 786436 | tf_op jit(solution)/shard_map/while
  171.8 1.7 copy-start.2
  175.4 3.7 copy-start.7
  179.1 6.7 %copy-start.6 = (bf16[4,256,128]{2,1,0:T(8,128)(2,1)}, bf16[4,256,128]{2,1,0:T(8,128)(2,1)S(1)}, u32[]{:S(2)}) copy-start(bf16[4,256,128]{2,1,0:T(8,128)(2,1)S(1)} %get-tuple-element.314) | copy-start | bytes 786436 | tf_op jit(solution)/shard_map/while
  184.0 1.7 copy-start.2
  187.6 3.6 copy-start.7
  192.0 185.6 %reduce-scatter.4.cloned.1.call-start = ((), (), s32[]{:S(2)}) async-start(), calls=%async_computation.3 | async-start | bytes 6553600
  192.3 27.5 %copy-start.5 = (bf16[1024,256]{1,0:T(8,128)(2,1)S(1)}, bf16[1024,256]{1,0:T(8,128)(2,1)}, u32[]{:S(2)}) copy-start(bf16[1024,256]{1,0:T(8,128)(2,1)} %copy-done.4) | copy-start | bytes 1572868
  230.2 27.3 %copy-start.11 = (f32[1280]{0:T(1024)S(1)}, f32[1280]{0:T(1024)}, u32[]{:S(2)}) copy-start(f32[1280]{0:T(1024)} %param.31) | copy-start | bytes 15364
  278.2 102.4 %copy-start.1 = (bf16[2560,256]{1,0:T(8,128)(2,1)S(1)}, bf16[2560,256]{1,0:T(8,128)(2,1)}, u32[]{:S(2)}) copy-start(bf16[2560,256]{1,0:T(8,128)(2,1)} %param.22) | copy-start | bytes 3932164
Sparse Core Ops, SparseCore 0:
  9.6 100.7 all-gather.4
  192.2 27.4 all-gather.6
  278.4 99.2 reduce-scatter.3
where the time goes:
time: 390 us; the launch traced here: 387 us
  waiting for transfers between devices  149 us (38%)
  blocking collectives  74.8 us (19%)
  matrix products  67.1 us (17%)
  local copies, waits for them, and re-layouts  37.9 us (10%)
  other arithmetic  36.9 us (9%)
  between operations  15.3 us (4%)
  starting transfers between devices  5.96 us (2%)
    all_gather x1, waiting for transfers between devices, shards(): piece = lax.all_gather(hidden, 'tp', axis=1, tiled=True)  100 us
    pmax x1, blocking collectives, shards(): peak_value = lax.pmax(jnp.max(jnp.abs(normed)), ('seq', 'tp'))  51 us
    unnamed x4, waiting for transfers between devices  43.9 us
    dot_general x4, matrix products, shards(): jnp.dot(piece, matrix, preferred_element_type=jnp.float32)  31.9 us
    dot_general x1, matrix products, shards(): partial_value = jnp.dot(quant, out_proj, preferred_element_type=jnp.float32)  12.8 us
    unnamed x34, local copies, waits for them, and re-layouts  12.1 us
    unnamed x1, blocking collectives  12.1 us
    psum x1, blocking collectives, shards(): squares = lax.psum(local_squares, 'tp')  11.7 us
  transfers between devices with their start and end apart: 5, of which 3 were waited for; matrix products, arithmetic and copies ran while one was open for 8% of the time, Pallas kernels for 0%

commit v1 on v0

--- a/solution.py
+++ b/solution.py
@@ -99,7 +99,12 @@
     head_width = inner_local // head_count
     kernel = conv_weight.shape[0]
     matrices = (gate_proj, input_proj, bc_proj, step_proj)
-    piece = lax.all_gather(hidden, "tp", axis=1, tiled=True)
+    ring = [hidden]
+    for hop in range(3):
+        ring.append(lax.ppermute(ring[-1], "tp", [(dev, (dev + 1) % 4) for dev in range(4)]))
+    piece = jnp.roll(
+        jnp.concatenate(ring[::-1], axis=1), (lax.axis_index("tp") + 1) * ring[0].shape[1], axis=1
+    )
     gate_raw, x_raw, bc_raw, step_raw = tuple(
         (jnp.dot(piece, matrix, preferred_element_type=jnp.float32) for matrix in matrices)
     )

time: 390 us -> 390 us (level)
  local copies, waits for them, and re-layouts: 37.9 us -> 47 us
  waiting for transfers between devices: 149 us -> 140 us
    all_gather x1 -> x0, waiting for transfers between devices: 100 us -> none  [shards(): piece = lax.all_gather(hidden, 'tp', axis=1, tiled=True)]
    ppermute x0 -> x3, waiting for transfers between devices: none -> 91 us  [shards(): lax.ppermute(ring[-1], 'tp', [(dev, (dev + 1) % 4) for dev in range(4)])]
    unnamed x34 -> x51, local copies, waits for them, and re-layouts: 12.1 us -> 20.3 us
    unnamed x4 -> x3, waiting for transfers between devices: 43.9 us -> 43.2 us
  transfers between devices with their start and end apart: 5 -> 7, of which waited for: 3 -> 5; matrix products, arithmetic and copies ran while one was open for 8% -> 9% of each run, Pallas kernels for 0% -> 0%
where the time goes in v1:
time: 390 us; the launch traced here: 387 us
  waiting for transfers between devices  140 us (36%)
  blocking collectives  74.5 us (19%)
  matrix products  66.9 us (17%)
  local copies, waits for them, and re-layouts  47 us (12%)
  other arithmetic  34 us (9%)
  between operations  15.8 us (4%)
  starting transfers between devices  8.35 us (2%)
    ppermute x3, waiting for transfers between devices, shards(): lax.ppermute(ring[-1], 'tp', [(dev, (dev + 1) % 4) for dev in range(4)])  91 us
    pmax x1, blocking collectives, shards(): peak_value = lax.pmax(jnp.max(jnp.abs(normed)), ('seq', 'tp'))  51 us
    unnamed x3, waiting for transfers between devices  43.2 us
    dot_general x4, matrix products, shards(): jnp.dot(piece, matrix, preferred_element_type=jnp.float32)  31.8 us
    unnamed x51, local copies, waits for them, and re-layouts  20.3 us
    dot_general x1, matrix products, shards(): partial_value = jnp.dot(quant, out_proj, preferred_element_type=jnp.float32)  12.7 us
    unnamed x1, blocking collectives  11.9 us
    psum x1, blocking collectives, shards(): squares = lax.psum(local_squares, 'tp')  11.6 us
  transfers between devices with their start and end apart: 7, of which 5 were waited for; matrix products, arithmetic and copies ran while one was open for 9% of the time, Pallas kernels for 0%

profile of v1, /device:TPU:0, one launch (start us, length us, event | category | flops | bytes accessed | tf_op | source)
XLA Modules:
  0.0 387.2 jit_solution(15589827454237731181)
XLA Ops:
  7.2 3.1 collective-permute-start
  10.3 31.0 %collective-permute-done = bf16[1024,640]{1,0:T(8,128)(2,1)S(1)} collective-permute-done((bf16[1024,640]{1,0:T(8,128)(2,1)}, bf16[1024,640]{1,0:T(8,128)(2,1)S(1)}, u32[]{:S(2)}, u32[]{:S(2)}) %collective-permute-start) | collective-permute-done | bytes 1310752 | tf_op jit(solution)/shard_map/ppermute | solution.py:104
  42.4 31.8 %collective-permute-done.1 = bf16[1024,640]{1,0:T(8,128)(2,1)} collective-permute-done((bf16[1024,640]{1,0:T(8,128)(2,1)S(1)}, bf16[1024,640]{1,0:T(8,128)(2,1)}, u32[]{:S(2)}, u32[]{:S(2)}) %collective-permute-start.1) | collective-permute-done | bytes 1310752 | tf_op jit(solution)/shard_map/ppermute | solution.py:104
  74.3 1.5 slice_reduce_fusion.5
  77.3 28.2 %collective-permute-done.2 = bf16[1024,640]{1,0:T(8,128)(2,1)} collective-permute-done((bf16[1024,640]{1,0:T(8,128)(2,1)}, bf16[1024,640]{1,0:T(8,128)(2,1)}, u32[]{:S(2)}, u32[]{:S(2)}) %collective-permute-start.2) | collective-permute-done | bytes 1310752 | tf_op jit(solution)/shard_map/ppermute | solution.py:104
  105.5 1.5 constant_dynamic-update-slice_fusion.8
  107.0 1.6 constant_dynamic-update-slice_fusion.7
  109.1 1.6 constant_dynamic-update-slice_fusion.4
  110.7 1.6 constant_dynamic-update-slice_fusion.3
  112.9 2.2 fusion.45
  116.4 2.9 fusion.54
  120.2 11.1 %convolution_convert_fusion.2 = bf16[1024,1280]{1,0:T(8,128)(2,1)S(1)} fusion(bf16[2560,1280]{1,0:T(8,128)(2,1)} %param.21, bf16[1024,5120]{1,0:T(8,128)(2,1)} %copy-done.10, s32[]{:T(128)S(6)} %select_n.35), kind=kOutput, calls=%fused_computation.58 | convolution fusion | flops 6712197120 | bytes 14417924 | tf_op jit(solution)/shard_map/dot_general | solution.py:109
  131.3 3.9 collective-permute-start.3
  136.8 4.7 %multiply_convert_fusion.4 = bf16[1024,1280]{1,0:T(8,128)(2,1)} fusion(bf16[1024,1280]{1,0:T(8,128)(2,1)S(1)} %convolution_convert_fusion.2, bf16[3,1280]{1,0:T(4,128)(2,1)S(1)} %collective-permute-done.3, f32[1280]{0:T(1024)S(1)} %copy-done.13, f32[1280]{0:T(1024)S(1)} %copy-done.11, f32[1280]{0:T(1024)S(1)} %copy-done.12, f32[1280]{0:T(1024)S(1)} %get-tuple-element.152, ...), kind=kLoop, calls=%fused_computation.56 | loop fusion | flops 34078720 | bytes 5276160 | tf_op jit(solution)/shard_map/convert_element_type | solution.py:45
  141.5 48.6 %while.26 = (s32[]{:T(128)}, f32[20,64,128]{2,1,0:T(8,128)S(1)}, f32[4,256,1280]{2,1,0:T(8,128)}, f32[4,20,256]{2,1,0:T(8,128)}, f32[4,20,256]{2,1,0:T(8,128)}, ...) while((s32[]{:T(128)}, f32[20,64,128]{2,1,0:T(8,128)S(1)}, ...), condition=%wide.region_3.4_spmd.clone, body=%wide.region_0.3_spmd.clone.sunk | while | flops 782641216 | bytes 22548344 | solution.py:132
  146.5 1.7 fusion.97
  158.7 1.7 fusion.97
  170.8 1.7 fusion.97
  183.0 1.7 fusion.97
  194.7 11.9 %all-reduce = bf16[160]{0:T(256)(128)(2,1)S(1)} all-reduce(bf16[160]{0:T(256)(128)(2,1)S(1)} %dynamic-update-slice), channel_id=2, replica_groups=mesh['seq'=8,'tp'=4] {'seq'}, use_global_device_ids=true, to_apply=%add | all-reduce | flops 160 | bytes 640
  207.6 5.6 %reduce-window.16 = f32[20,8,128]{2,1,0:T(8,128)S(1)} reduce-window(f32[20,8,128]{2,1,0:T(8,128)S(1)} %slice.113, f32[]{:T(128)} %constant.82.clone.1), window={size=1x1x128 pad=0_0x0_0x127_0}, to_apply=%region_4.5 | reduce-window | flops 2600960 | bytes 163844 | tf_op jit(solution)/shard_map/reduce-window.2
  213.8 5.5 %all-gather.4.cloned.1.call-done = bf16[160,64,128]{2,1,0:T(8,128)(2,1)} async-done(((bf16[20,64,128]{2,1,0:T(8,128)(2,1)}), bf16[160,64,128]{2,1,0:T(8,128)(2,1)}) %all-gather.4.cloned.1.call-update) | async-done | bytes 2621456 | tf_op jit(solution)/shard_map/all_gather | solution.py:21
  219.6 4.4 %broadcast_multiply_fusion = f32[1024,20,64]{0,2,1:T(8,128)} fusion(f32[1024,20]{0,1:T(8,128)S(1)} %bitcast.147, f32[20,64,128]{2,1,0:T(8,128)S(1)} %get-tuple-element.91, bf16[1024,256]{1,0:T(8,128)(2,1)S(1)} %copy-done.7), kind=kOutput, calls=%fused_computation.75 | convolution fusion | flops 2014576640 | bytes 6258688 | tf_op jit(solution)/shard_map/tn,hpn->thp/dot_general | solution.py:138
  224.0 6.0 %copy.53 = f32[1024,1280]{1,0:T(8,128)} copy(f32[1024,1280]{0,1:T(8,128)} %bitcast.135) | data formatting | bytes 10485760 | tf_op jit(solution)/shard_map/reshape | solution.py:141
  230.0 15.6 %multiply_reduce_fusion = (f32[1024]{0:T(1024)S(1)}, f32[1024,1280]{1,0:T(8,128)}) fusion(bf16[2560,1280]{1,0:T(8,128)(2,1)} %param.20, bf16[1024,5120]{1,0:T(8,128)(2,1)} %copy-done.10, s32[]{:T(128)S(6)} %select_n.35, bf16[1024,1280]{1,0:T(8,128)(2,1)} %bitcast.138, f32[1280]{0:T(1024)S(1)} %mul.251, f32[1024,1280]{1,0:T(8,128)} %copy.53, ...), kind=kOutput, calls=%fused_computation.55 | convolution fusion | flops 6727924736 | bytes 30155780 | tf_op jit(solution)/shard_map/dot_general | solution.py:109
  245.6 11.6 %psum.7 = f32[1024]{0:T(1024)S(1)} all-reduce(f32[1024]{0:T(1024)S(1)} %get-tuple-element.195), channel_id=1, replica_groups=mesh['seq'=8,'tp'=4] {'tp'}, use_global_device_ids=true, to_apply=%region_10.11 | all-reduce | flops 1024 | bytes 8192 | tf_op jit(solution)/shard_map/psum | solution.py:148
  257.2 12.7 %convolution_convert_fusion = bf16[1024,2560]{1,0:T(8,128)(2,1)} fusion(bf16[1280,2560]{1,0:T(8,128)(2,1)} %param.32, f32[1024,1280]{1,0:T(8,128)} %get-tuple-element.196, f32[]{:T(128)S(6)} %div.31, f32[1280]{0:T(1024)S(1)} %copy-done.14, f32[1024]{0:T(1024)S(1)} %add_rsqrt_fusion), kind=kOutput, calls=%fused_computation.45 | convolution fusion | flops 6720061440 | bytes 17048580 | tf_op jit(solution)/shard_map/dot_general | solution.py:154
  270.0 8.0 %copy.54 = bf16[1024,2560]{0,1:T(8,128)(2,1)} copy(bf16[1024,2560]{1,0:T(8,128)(2,1)} %convolution_convert_fusion) | data formatting | bytes 10485760
  278.0 4.0 %abs_reduce_fusion = f32[]{:T(128)} fusion(f32[1024,1280]{1,0:T(8,128)} %get-tuple-element.196, f32[1280]{0:T(1024)S(1)} %copy-done.14, f32[1024]{0:T(1024)S(1)} %add_rsqrt_fusion), kind=kLoop, calls=%fused_computation.52 | loop fusion | flops 5242879 | bytes 5252100 | tf_op jit(solution)/shard_map/reduce_max | solution.py:151
  281.9 51.0 %pmax.7 = f32[1]{0:T(128)} all-reduce(f32[1]{0:T(128)} %bitcast.19), channel_id=1, replica_groups=mesh['seq'=8,'tp'=4] {'seq','tp'}, use_global_device_ids=true, to_apply=%region_14.15 | all-reduce | flops 1 | bytes 8 | tf_op jit(solution)/shard_map/pmax | solution.py:151
  334.2 43.2 %reduce-scatter.4.cloned.1.call-done = bf16[640,1024]{1,0:T(8,128)(2,1)} async-done(((bf16[2560,1024]{1,0:T(8,128)(2,1)}), bf16[640,1024]{1,0:T(8,128)(2,1)}) %reduce-scatter.4.cloned.1.call-update) | async-done | bytes 1310736
  377.4 1.7 copy.55
  (200 shorter events, 56.2 us)
Async XLA Ops:
  7.2 105.7 %copy-start = (bf16[2560,256]{1,0:T(8,128)(2,1)S(1)}, bf16[2560,256]{1,0:T(8,128)(2,1)}, u32[]{:S(2)}) copy-start(bf16[2560,256]{1,0:T(8,128)(2,1)} %param.22) | copy-start | bytes 3932164
  7.2 101.7 %copy-start.3 = (bf16[1024,640]{1,0:T(8,128)(2,1)S(1)}, bf16[1024,640]{1,0:T(8,128)(2,1)}, u32[]{:S(2)}) copy-start(bf16[1024,640]{1,0:T(8,128)(2,1)} %param.19) | copy-start | bytes 3932164
  7.2 212.1 %all-gather.4.cloned.1.call-start = ((), (), s32[]{:S(2)}) async-start(), calls=%async_computation.1 | async-start | bytes 2949120 | tf_op jit(solution)/shard_map/all_gather | solution.py:21
  7.2 34.1 %collective-permute-start = (bf16[1024,640]{1,0:T(8,128)(2,1)}, bf16[1024,640]{1,0:T(8,128)(2,1)S(1)}, u32[]{:S(2)}, u32[]{:S(2)}) collective-permute-start(bf16[1024,640]{1,0:T(8,128)(2,1)} %param.19), channel_id=1, source_target_pairs={{0,1},{1,2},{2,3},{3,0},{4,5},{5,6},{6,7},{7,4},{8,9},{9,10},{10,1... | collective-permute-start | bytes 3932168 | tf_op jit(solution)/shard_map/ppermute | solution.py:104
  42.4 31.8 %collective-permute-start.1 = (bf16[1024,640]{1,0:T(8,128)(2,1)S(1)}, bf16[1024,640]{1,0:T(8,128)(2,1)}, u32[]{:S(2)}, u32[]{:S(2)}) collective-permute-start(bf16[1024,640]{1,0:T(8,128)(2,1)S(1)} %collective-permute-done), channel_id=1, source_target_pairs={{0,1},{1,2},{2,3},{3,0},{4,5},{5,6},{6,7},{7,4},{8,9},{9,10},{10,1... | collective-permute-start | bytes 3932168 | tf_op jit(solution)/shard_map/ppermute | solution.py:104
  74.3 31.2 %collective-permute-start.2 = (bf16[1024,640]{1,0:T(8,128)(2,1)}, bf16[1024,640]{1,0:T(8,128)(2,1)}, u32[]{:S(2)}, u32[]{:S(2)}) collective-permute-start(bf16[1024,640]{1,0:T(8,128)(2,1)} %collective-permute-done.1), channel_id=1, source_target_pairs={{0,1},{1,2},{2,3},{3,0},{4,5},{5,6},{6,7},{7,4},{8,9},{9,10},{10,1... | collective-permute-start | bytes 3932168 | tf_op jit(solution)/shard_map/ppermute | solution.py:104
  74.3 34.3 %copy-start.5 = (bf16[1024,640]{1,0:T(8,128)(2,1)S(1)}, bf16[1024,640]{1,0:T(8,128)(2,1)}, u32[]{:S(2)}) copy-start(bf16[1024,640]{1,0:T(8,128)(2,1)} %copy-done.4) | copy-start | bytes 3932164
  112.8 6.4 %copy-start.10 = (bf16[1024,5120]{1,0:T(8,128)(2,1)}, bf16[1024,5120]{1,0:T(8,128)(2,1)S(1)}, u32[]{:S(2)}) copy-start(bf16[1024,5120]{1,0:T(8,128)(2,1)S(1)} %constant_dynamic-update-slice_fusion.1) | copy-start | bytes 31457284
  112.8 3.5 copy-start.18
  112.9 3.5 copy-start.19
  115.1 20.9 %collective-permute-start.4 = (bf16[3,256]{1,0:T(4,128)(2,1)S(1)}, bf16[3,256]{1,0:T(4,128)(2,1)S(1)}, u32[]{:S(2)}, u32[]{:S(2)}) collective-permute-start(bf16[3,256]{1,0:T(4,128)(2,1)S(1)} %slice.104), channel_id=1, source_target_pairs={{0,4},{4,8},{8,12},{12,16},{16,20},{20,24},{24,28},{1,5},{5,9},{9,... | collective-permute-start | bytes 4616 | tf_op jit(solution)/shard_map/ppermute | solution.py:15
  120.1 15.8 %copy-start.15 = (f32[256]{0:T(256)S(1)}, f32[256]{0:T(256)}, u32[]{:S(2)}) copy-start(f32[256]{0:T(256)} %param.29) | copy-start | bytes 3076
  120.1 16.6 %copy-start.11 = (f32[1280]{0:T(1024)S(1)}, f32[1280]{0:T(1024)}, u32[]{:S(2)}) copy-start(f32[1280]{0:T(1024)} %get-tuple-element.153) | copy-start | bytes 15364
  120.2 16.6 %copy-start.12 = (f32[1280]{0:T(1024)S(1)}, f32[1280]{0:T(1024)}, u32[]{:S(2)}) copy-start(f32[1280]{0:T(1024)} %get-tuple-element.154) | copy-start | bytes 15364
  120.2 16.6 %copy-start.13 = (f32[1280]{0:T(1024)S(1)}, f32[1280]{0:T(1024)}, u32[]{:S(2)}) copy-start(f32[1280]{0:T(1024)} %param.27) | copy-start | bytes 15364
  131.3 5.4 %collective-permute-start.3 = (bf16[3,1280]{1,0:T(4,128)(2,1)S(1)}, bf16[3,1280]{1,0:T(4,128)(2,1)S(1)}, u32[]{:S(2)}, u32[]{:S(2)}) collective-permute-start(bf16[3,1280]{1,0:T(4,128)(2,1)S(1)} %slice.99), channel_id=1, source_target_pairs={{0,4},{4,8},{8,12},{12,16},{16,20},{20,24},{24,28},{1,5},{5,9},{9,... | collective-permute-start | bytes 23048 | tf_op jit(solution)/shard_map/ppermute | solution.py:15
  136.7 4.8 %copy-start.6 = (bf16[1024,256]{1,0:T(8,128)(2,1)}, bf16[1024,256]{1,0:T(8,128)(2,1)S(1)}, u32[]{:S(2)}) copy-start(bf16[1024,256]{1,0:T(8,128)(2,1)S(1)} %multiply_convert_fusion.5) | copy-start | bytes 1572868
  141.5 49.5 %copy-start.17 = (f32[20]{0:T(128)S(1)}, f32[20]{0:T(128)}, u32[]{:S(2)}) copy-start(f32[20]{0:T(128)} %param.30) | copy-start | bytes 244
  141.5 51.6 %copy-start.20 = (f32[16]{0:T(128)S(1)}, f32[16]{0:T(128)}, u32[]{:S(2)}) copy-start(f32[16]{0:T(128)} %param.33) | copy-start | bytes 196
  141.5 53.0 %copy-start.16 = (bf16[20]{0:T(256)(128)(2,1)S(1)}, bf16[20]{0:T(256)(128)(2,1)}, u32[]{:S(2)}) copy-start(bf16[20]{0:T(256)(128)(2,1)} %get-tuple-element.183) | copy-start | bytes 124
  141.5 6.7 %copy-start.8 = (bf16[4,256,128]{2,1,0:T(8,128)(2,1)}, bf16[4,256,128]{2,1,0:T(8,128)(2,1)S(1)}, u32[]{:S(2)}) copy-start(bf16[4,256,128]{2,1,0:T(8,128)(2,1)S(1)} %get-tuple-element.314) | copy-start | bytes 786436 | tf_op jit(solution)/shard_map/while
  150.0 3.6 copy-start.9
  153.7 6.7 %copy-start.8 = (bf16[4,256,128]{2,1,0:T(8,128)(2,1)}, bf16[4,256,128]{2,1,0:T(8,128)(2,1)S(1)}, u32[]{:S(2)}) copy-start(bf16[4,256,128]{2,1,0:T(8,128)(2,1)S(1)} %get-tuple-element.314) | copy-start | bytes 786436 | tf_op jit(solution)/shard_map/while
  162.2 3.6 copy-start.9
  165.9 6.7 %copy-start.8 = (bf16[4,256,128]{2,1,0:T(8,128)(2,1)}, bf16[4,256,128]{2,1,0:T(8,128)(2,1)S(1)}, u32[]{:S(2)}) copy-start(bf16[4,256,128]{2,1,0:T(8,128)(2,1)S(1)} %get-tuple-element.314) | copy-start | bytes 786436 | tf_op jit(solution)/shard_map/while
  174.4 3.6 copy-start.9
  178.0 6.7 %copy-start.8 = (bf16[4,256,128]{2,1,0:T(8,128)(2,1)}, bf16[4,256,128]{2,1,0:T(8,128)(2,1)S(1)}, u32[]{:S(2)}) copy-start(bf16[4,256,128]{2,1,0:T(8,128)(2,1)S(1)} %get-tuple-element.314) | copy-start | bytes 786436 | tf_op jit(solution)/shard_map/while
  186.5 3.6 copy-start.9
  190.9 186.4 %reduce-scatter.4.cloned.1.call-start = ((), (), s32[]{:S(2)}) async-start(), calls=%async_computation.2 | async-start | bytes 6553600
  191.0 28.6 %copy-start.7 = (bf16[1024,256]{1,0:T(8,128)(2,1)S(1)}, bf16[1024,256]{1,0:T(8,128)(2,1)}, u32[]{:S(2)}) copy-start(bf16[1024,256]{1,0:T(8,128)(2,1)} %copy-done.6) | copy-start | bytes 1572868
  230.0 27.2 %copy-start.14 = (f32[1280]{0:T(1024)S(1)}, f32[1280]{0:T(1024)}, u32[]{:S(2)}) copy-start(f32[1280]{0:T(1024)} %param.31) | copy-start | bytes 15364
  277.9 102.4 %copy-start.1 = (bf16[2560,256]{1,0:T(8,128)(2,1)S(1)}, bf16[2560,256]{1,0:T(8,128)(2,1)}, u32[]{:S(2)}) copy-start(bf16[2560,256]{1,0:T(8,128)(2,1)} %param.22) | copy-start | bytes 3932164
  (5 other events, 8.0 us)
Sparse Core Ops, SparseCore 0:
  191.1 28.1 all-gather.3
  278.1 99.2 reduce-scatter.3
